TPU v7x, 256 devices: a whole 4x4x8 slice. The times are simulated.
256 devices in a mesh: grp: 16 (over y, z_lo, core), seq: 16 (over x, z_hi).
Axes of the slice: x: 4, y: 4, z: 8 (z_hi: 4, z_lo: 2; z = z_hi * 2 + z_lo), core: 2. Of those that a mesh axis runs over, the one named last changes fastest.
Arguments:
- prefix_hidden: bfloat16 [16, 2048, 5120], P('grp', 'seq'), may hold values from -6 to 6
- prefix_keys: bfloat16 [16, 2048, 512], P('grp', 'seq'), may hold values from -6 to 6
- prefix_value_rows: bfloat16 [16, 2048, 512], P('grp', 'seq'), may hold values from -6 to 6
- comp_hidden: bfloat16 [16, 256, 5120], P('grp', 'seq'), may hold values from -6 to 6
- completion_queries: bfloat16 [16, 256, 2560], P('grp', 'seq'), may hold values from -6 to 6
- completion_keys: bfloat16 [16, 256, 512], P('grp', 'seq'), may hold values from -6 to 6
- completion_values: bfloat16 [16, 256, 512], P('grp', 'seq'), may hold values from -6 to 6
- out_grad: bfloat16 [16, 256, 2560], P('grp', 'seq'), may hold values from -6 to 6
- counts: int32 [16], P('grp'), may hold values from 4 to 16
- lengths: int32 [16, 16], P('grp', 'seq'), may hold values from 1 to 16
Outputs:
- attn_out: bfloat16 [16, 256, 2560], P('grp', 'seq')
- completion_query_gradient: bfloat16 [16, 256, 2560], P('grp', 'seq')
- comp_key_grad: bfloat16 [16, 256, 512], P('grp', 'seq')
- comp_value_grad: bfloat16 [16, 256, 512], P('grp', 'seq')
- prefix_key_grad: bfloat16 [16, 2048, 512], P('grp', 'seq')
- prefix_value_grad: bfloat16 [16, 2048, 512], P('grp', 'seq')
- value_proj_grad: float32 [5120, 512], P('seq')
Inputs may be any that keep to these rules, and one draw needn't show every extreme that they name: Completion slots 0 to counts[g] - 1 of group g carry a completion; the others are empty. A completion occupies the first lengths[g, c] token slots of its slot.
All inputs are finite; a program needn't handle non-finite values.
Results may differ from a plain program's by a relative error of at most 0.013.
The roundings to bfloat16 on the way count: a program that leaves them out, or rounds other values in their place, can miss the bound.
Values may be sent and summed in bfloat16 or wider, within the bound.
No kernel may reach another device: no remote copies, remote signals or barrier semaphores. Data moves between devices by JAX's collectives and lax.ppermute only.
A program may use at most 64 MiB of HBM per device.

v0:
```python
import jax
import jax.numpy as jnp
from jax import lax
from jax.sharding import PartitionSpec as P

HEAD_SIZE = 128
QUERY_HEADS = 20
KEY_VALUE_HEADS = 4
SLOT_LENGTH = 16
LOCAL_COMPLETION = 1


NEG_BIG = -1e30


def sent_together(arrays, axis, dim, along):
    widths = [a.shape[along] for a in arrays]
    both = jnp.concatenate(arrays, axis=along)
    whole = lax.all_gather(both, axis, axis=dim, tiled=True)
    return tuple(jnp.split(whole, [sum(widths[:k]) for k in range(1, len(widths))], axis=along))


def in_order(parts, dim):
    dims = list(parts.shape[1:])
    dims[dim] *= parts.shape[0]
    return jnp.moveaxis(parts, 0, dim).reshape(dims)


def gather_together(arrays, axis, dims):
    flat = jnp.concatenate([a.reshape(-1) for a in arrays])
    lines, at, finished = (lax.all_gather(flat, axis), 0, [])
    for a, dim in zip(arrays, dims):
        parts = lines[:, at : at + a.size].reshape(-1, *a.shape)
        finished.append(in_order(parts, dim))
        at += a.size
    return tuple(finished)


def over_pieces(array, axis):
    return lax.all_gather(array, axis).sum(0)


def block_count(total):
    return total // 512


def divided_blocks(rows):
    count = block_count(rows.shape[0])
    return rows.reshape((count, rows.shape[0] // count) + rows.shape[1:])


def to_rows(values):
    return jnp.transpose(values, (1, 2, 0, 3)).reshape(values.shape[1], values.shape[2], -1)


def from_rows(values, comps):
    return jnp.transpose(values.reshape(values.shape[0], values.shape[1], comps, -1), (2, 0, 1, 3))


def transposed_dot(left, right):
    return lax.dot_general(
        left.astype(jnp.float32),
        right,
        (((0,), (0,)), ((), ())),
        precision=lax.Precision.HIGHEST,
        preferred_element_type=jnp.float32,
    )


def per_device(
    prefix_hidden,
    prefix_keys,
    prefix_value_rows,
    comp_hidden,
    completion_queries,
    completion_keys,
    completion_values,
    out_grad,
    counts,
    lengths,
):
    head_repeat = QUERY_HEADS // KEY_VALUE_HEADS
    token_rows = LOCAL_COMPLETION * SLOT_LENGTH
    key_value_width = KEY_VALUE_HEADS * HEAD_SIZE
    scale = HEAD_SIZE ** (-0.5)
    query_rows = completion_queries[0].reshape(token_rows, KEY_VALUE_HEADS, head_repeat, HEAD_SIZE)
    slot = jnp.arange(token_rows) // SLOT_LENGTH
    posit = jnp.arange(token_rows) % SLOT_LENGTH
    slot_len = jnp.sum(
        jnp.where(slot[:, None] == jnp.arange(LOCAL_COMPLETION)[None, :], lengths[0][None, :], 0),
        axis=1,
    )
    first_slot = lax.axis_index("seq") * LOCAL_COMPLETION
    live_mask = ((first_slot + slot < counts[0]) & (posit < slot_len)).astype(jnp.float32)
    output_gradient = (
        (out_grad[0].astype(jnp.float32) * live_mask[:, None])
        .astype(jnp.bfloat16)
        .reshape(token_rows, KEY_VALUE_HEADS, head_repeat, HEAD_SIZE)
    )
    completion_query_rows = query_rows.reshape(
        LOCAL_COMPLETION, SLOT_LENGTH, KEY_VALUE_HEADS, head_repeat, HEAD_SIZE
    )
    completion_key_rows = completion_keys[0].reshape(
        LOCAL_COMPLETION, SLOT_LENGTH, KEY_VALUE_HEADS, HEAD_SIZE
    )
    completion_value_rows = completion_values[0].reshape(
        LOCAL_COMPLETION, SLOT_LENGTH, KEY_VALUE_HEADS, HEAD_SIZE
    )
    causal = jnp.arange(SLOT_LENGTH)[:, None] >= jnp.arange(SLOT_LENGTH)[None, :]
    own_raw = (
        jnp.einsum(
            "ctkrd,cukd->ckrtu",
            completion_query_rows,
            completion_key_rows,
            preferred_element_type=jnp.float32,
        )
        * scale
    )
    own_scores = jnp.where(causal, own_raw, NEG_BIG)
    own_max = jnp.max(own_scores, axis=-1)
    own_sum = jnp.sum(jnp.exp(own_scores - own_max[..., None]), axis=-1)
    stats = (to_rows(own_max), to_rows(own_sum))

    def scores_of(block):
        return (
            jnp.einsum("tkrd,jkd->krtj", query_rows, block, preferred_element_type=jnp.float32)
            * scale
        )

    def add_stats(carry, block):
        high, total = carry
        scores = scores_of(block)
        new_high = jnp.maximum(high, jnp.max(scores, axis=-1))
        new_total = total * jnp.exp(high - new_high) + jnp.sum(
            jnp.exp(scores - new_high[..., None]), axis=-1
        )
        return ((new_high, new_total), None)

    joined_keys, joined_values = sent_together((prefix_keys[0], prefix_value_rows[0]), "seq", 0, 1)
    carry = stats
    block_list = divided_blocks(
        joined_keys.reshape(joined_keys.shape[0], KEY_VALUE_HEADS, HEAD_SIZE)
    )
    carry, unused = lax.scan(add_stats, carry, block_list)
    stats = carry
    lse = stats[0] + jnp.log(stats[1])
    key_block_list = divided_blocks(
        joined_keys.reshape(joined_keys.shape[0], KEY_VALUE_HEADS, HEAD_SIZE)
    )
    value_block_list = divided_blocks(
        joined_values.reshape(joined_values.shape[0], KEY_VALUE_HEADS, HEAD_SIZE)
    )
    own_probs = jnp.exp(own_scores - from_rows(lse, LOCAL_COMPLETION)[..., None])
    own_weights_narrow = own_probs.astype(jnp.bfloat16)
    context_rows = jnp.einsum(
        "xsgav,xvsh->xasgh",
        own_weights_narrow,
        completion_value_rows,
        preferred_element_type=jnp.float32,
    )
    context_rows = context_rows.reshape(token_rows, KEY_VALUE_HEADS, head_repeat, HEAD_SIZE)

    def add_context(total, pair):
        probs = jnp.exp(scores_of(pair[0]) - lse[..., None]).astype(jnp.bfloat16)
        return (
            total
            + jnp.einsum("krtj,jkd->tkrd", probs, pair[1], preferred_element_type=jnp.float32),
            None,
        )

    context_rows, unused = lax.scan(add_context, context_rows, (key_block_list, value_block_list))
    attn_out = (
        (context_rows * live_mask[:, None, None, None])
        .astype(jnp.bfloat16)
        .reshape(1, token_rows, QUERY_HEADS * HEAD_SIZE)
    )
    delta = jnp.transpose(
        jnp.sum(output_gradient.astype(jnp.float32) * context_rows, axis=-1), (1, 2, 0)
    )
    completion_output_gradient = output_gradient.reshape(
        LOCAL_COMPLETION, SLOT_LENGTH, KEY_VALUE_HEADS, head_repeat, HEAD_SIZE
    )
    own_dprob = jnp.einsum(
        "ctkrd,cukd->ckrtu",
        completion_output_gradient,
        completion_value_rows,
        preferred_element_type=jnp.float32,
    )
    own_ds_b = (own_probs * (own_dprob - from_rows(delta, LOCAL_COMPLETION)[..., None])).astype(
        jnp.bfloat16
    )
    own_query_gradient = (
        jnp.einsum(
            "xsgav,xvsh->xasgh", own_ds_b, completion_key_rows, preferred_element_type=jnp.float32
        )
        * scale
    )
    dk_own = (
        jnp.einsum(
            "ckrtu,ctkrd->cukd", own_ds_b, completion_query_rows, preferred_element_type=jnp.float32
        )
        * scale
    )
    dv_own = jnp.einsum(
        "ckrtu,ctkrd->cukd",
        own_weights_narrow,
        completion_output_gradient,
        preferred_element_type=jnp.float32,
    )

    def prefix_update(total, pair):
        probs = jnp.exp(scores_of(pair[0]) - lse[..., None])
        probs_b = probs.astype(jnp.bfloat16)
        dprob = jnp.einsum(
            "tkrd,jkd->krtj", output_gradient, pair[1], preferred_element_type=jnp.float32
        )
        dscore_b = (probs * (dprob - delta[..., None])).astype(jnp.bfloat16)
        total = (
            total
            + jnp.einsum("krtj,jkd->tkrd", dscore_b, pair[0], preferred_element_type=jnp.float32)
            * scale
        )
        key_part = (
            jnp.einsum("krtj,tkrd->jkd", dscore_b, query_rows, preferred_element_type=jnp.float32)
            * scale
        )
        value_part = jnp.einsum(
            "krtj,tkrd->jkd", probs_b, output_gradient, preferred_element_type=jnp.float32
        )
        rows = pair[0].shape[0]
        return (
            total,
            jnp.concatenate([key_part.reshape(rows, -1), value_part.reshape(rows, -1)], axis=1),
        )

    prefix_query_gradient, gradient_blocks = lax.scan(
        prefix_update,
        jnp.zeros((token_rows, KEY_VALUE_HEADS, head_repeat, HEAD_SIZE), jnp.float32),
        (key_block_list, value_block_list),
    )
    grad_terms = gradient_blocks.reshape(-1, 2 * key_value_width)
    prefix_grad = lax.psum_scatter(grad_terms, "seq", scatter_dimension=0, tiled=True)
    completion_query_gradient = (
        (
            prefix_query_gradient
            + own_query_gradient.reshape(token_rows, KEY_VALUE_HEADS, head_repeat, HEAD_SIZE)
        )
        .astype(jnp.bfloat16)
        .reshape(1, token_rows, QUERY_HEADS * HEAD_SIZE)
    )
    value_terms_comp = dv_own.reshape(token_rows, key_value_width)
    value_terms_pre = prefix_grad[:, key_value_width:]
    comp_value_b = value_terms_comp.astype(jnp.bfloat16)
    comp_key_grad = dk_own.reshape(1, token_rows, key_value_width).astype(jnp.bfloat16)
    prefix_key_b = prefix_grad[:, :key_value_width].astype(jnp.bfloat16)
    prefix_value_b = value_terms_pre.astype(jnp.bfloat16)
    hidden_pre = prefix_hidden[0]
    hidden_comp = comp_hidden[0]
    cols_pre, cols_comp = (
        lax.all_to_all(hidden_pre, "seq", split_axis=1, concat_axis=0, tiled=True),
        lax.all_to_all(hidden_comp, "seq", split_axis=1, concat_axis=0, tiled=True),
    )
    grads_pre, grads_comp = gather_together((value_terms_pre, value_terms_comp), "seq", (0, 0))
    proj_share = transposed_dot(cols_pre, grads_pre) + transposed_dot(cols_comp, grads_comp)
    value_proj_grad = over_pieces(proj_share, "grp")
    return (
        attn_out,
        completion_query_gradient,
        comp_key_grad,
        comp_value_b.reshape(1, token_rows, key_value_width),
        prefix_key_b[None],
        prefix_value_b[None],
        value_proj_grad,
    )


def solution(mesh):
    in_specs = (
        P("grp", "seq", None),
        P("grp", "seq", None),
        P("grp", "seq", None),
        P("grp", "seq", None),
        P("grp", "seq", None),
        P("grp", "seq", None),
        P("grp", "seq", None),
        P("grp", "seq", None),
        P("grp"),
        P("grp", "seq"),
    )
    out_specs = (
        P("grp", "seq", None),
        P("grp", "seq", None),
        P("grp", "seq", None),
        P("grp", "seq", None),
        P("grp", "seq", None),
        P("grp", "seq", None),
        P("seq", None),
    )
    return jax.shard_map(
        per_device, mesh=mesh, in_specs=in_specs, out_specs=out_specs, check_vma=False
    )
```

profile of v0, /device:TPU:1, one launch (start us, length us, event | category | flops | bytes accessed | tf_op | source)
XLA Modules:
  0.0 487.8 jit_solution(5156677914569723918)
XLA Ops:
  7.2 1.7 pad_maximum_fusion.1
  14.2 75.1 %all-gather.6.cloned.1.call-done = bf16[2048,1024]{1,0:T(8,128)(2,1)} async-done(((bf16[128,1024]{1,0:T(8,128)(2,1)}), bf16[2048,1024]{1,0:T(8,128)(2,1)}) %all-gather.6.cloned.1.call-update) | async-done | bytes 4194320 | tf_op jit(solution)/shard_map/all_gather | solution.py:19
  89.3 4.4 fusion.71
  93.7 2.5 reshape_reshape.17
  96.3 1.7 copy.58
  98.0 7.0 %while.35 = (s32[]{:T(128)}, f32[4,5,16]{2,1,0:T(8,128)S(1)}, f32[4,5,16]{2,1,0:T(8,128)S(1)}, bf16[4,512,4,128]{3,1,2,0:T(8,128)(2,1)}, bf16[16,4,5,128]{3,0,2,1:T(8,128)(2,1)S(1)}, /*index=5*/s32[]{:T(128)}) while((s32[]{:T(128)}, f32[4,5,16]{2,1,0:T(8,128)S(1)}, f32[4,5,16]{2,1,0:T(8,128)S(1)}, bf16[4,512,4,128]{3,1,2,0:T(8,128)(2,1)}, ...), condition=%wide.region_5.6_spmd, body=%wide.region_2.5_spmd.sunk | while | flops 42599040 | bytes 1933649 | solution.py:144
  98.0 1.4 fusion.113
  99.8 1.4 fusion.113
  101.5 1.4 fusion.113
  103.3 1.4 fusion.113
  105.0 2.6 reshape_reshape.18
  107.6 1.7 copy.62
  109.5 6.7 %while.36 = (s32[]{:T(128)}, f32[16,4,5,128]{3,0,2,1:T(8,128)S(1)}, bf16[4,512,4,128]{3,1,2,0:T(8,128)(2,1)}, bf16[4,512,4,128]{3,1,2,0:T(8,128)(2,1)}, bf16[16,...) while((s32[]{:T(128)}, f32[16,4,5,128]{3,0,2,1:T(8,128)S(1)}, ...), condition=%wide.region_7.8_spmd, body=%wide.region_6.7_spmd.sunk | while | flops 84418560 | bytes 1460565 | solution.py:171
  109.5 1.7 fusion.117
  111.2 1.7 fusion.117
  112.9 1.7 fusion.117
  114.6 1.7 fusion.117
  116.6 38.6 %while.37 = (s32[]{:T(128)}, f32[16,4,5,128]{3,0,2,1:T(8,128)S(1)}, f32[4,512,1024]{2,1,0:T(8,128)}, bf16[4,512,4,128]{3,1,2,0:T(8,128)(2,1)}, bf16[16,4,5,128]{...) while((s32[]{:T(128)}, f32[16,4,5,128]{3,0,2,1:T(8,128)S(1)}, ...), condition=%wide.region_10.11_spmd.clone, body=%wide.region_9.10_spmd.clone.sunk | while | flops 211607552 | bytes 19860112 | solution.py:236
  116.6 1.4 fusion.128
  118.0 1.4 fusion.129
  121.4 1.5 maximum_bitcast_fusion.2
  122.9 1.9 copy.145
  124.8 1.5 constant_dynamic-update-slice_fusion.2
  127.7 1.4 fusion.129
  131.1 1.5 maximum_bitcast_fusion.2
  132.6 1.9 copy.145
  134.5 1.5 constant_dynamic-update-slice_fusion.2
  137.3 1.4 fusion.129
  140.7 1.5 maximum_bitcast_fusion.2
  142.2 1.9 copy.145
  144.1 1.5 constant_dynamic-update-slice_fusion.2
  145.6 1.4 fusion.128
  147.0 1.4 fusion.129
  150.4 1.5 maximum_bitcast_fusion.2
  151.9 1.9 copy.145
  153.8 1.5 constant_dynamic-update-slice_fusion.2
  155.6 121.0 %reduce-scatter.2.cloned.1.call-done = f32[128,1024]{1,0:T(8,128)} async-done(((f32[2048,1024]{1,0:T(8,128)}), f32[128,1024]{1,0:T(8,128)}) %reduce-scatter.2.cloned.1.call-update) | async-done | bytes 524304 | tf_op jit(solution)/shard_map/reduce_scatter | solution.py:242
  278.4 1.5 copy.85
  279.9 7.4 %all-to-all-start = ((bf16[128,16,320]{0,2,1:T(8,128)(2,1)}), bf16[128,16,320]{0,2,1:T(8,128)(2,1)S(1)}, u32[]{:S(2)}, u32[]{:S(2)}) async-start(bf16[128,16,320]{0,2,1:T(8,128)(2,1)} %bitcast.50), calls=%async_computation.1 | async-start | bytes 2621440 | tf_op jit(solution)/shard_map/all_to_all | solution.py:260
  288.2 89.9 %all-gather.8.cloned.1.call-done = f32[1179648]{0:T(1024)} async-done(((f32[73728]{0:T(1024)}), f32[1179648]{0:T(1024)}) %all-gather.8.cloned.1.call-update) | async-done | bytes 4718608 | tf_op jit(solution)/shard_map/all_gather | solution.py:31
  378.1 4.2 reshape.231
  382.3 4.5 slice.19
  386.8 4.1 reshape_reshape.20
  391.7 9.9 %all-to-all-start.1 = ((bf16[16,16,320]{2,0,1:T(8,128)(2,1)}), bf16[16,16,320]{2,0,1:T(8,128)(2,1)S(1)}, u32[]{:S(2)}, u32[]{:S(2)}) async-start(bf16[16,16,320]{2,0,1:T(8,128)(2,1)} %copy.87), calls=%async_computation.2 | async-start | bytes 393216 | tf_op jit(solution)/shard_map/all_to_all | solution.py:261
  401.9 4.6 fusion.42
  406.6 6.2 %all-to-all-done.1 = bf16[16,16,320]{2,0,1:T(8,128)(2,1)S(1)} async-done(((bf16[16,16,320]{2,0,1:T(8,128)(2,1)}), bf16[16,16,320]{2,0,1:T(8,128)(2,1)S(1)}, u32[]{:S(2)}, u32[]{:S(2)}) %all-to-all-start.1) | async-done | bytes 163872 | tf_op jit(solution)/shard_map/all_to_all | solution.py:261
  418.3 56.8 %all-gather.10.cloned.1.call-done = f32[5120,512]{1,0:T(8,128)} async-done(((f32[320,512]{1,0:T(8,128)}), f32[5120,512]{1,0:T(8,128)}) %all-gather.10.cloned.1.call-update) | async-done | bytes 10485776 | tf_op jit(solution)/shard_map/all_gather | solution.py:40
  475.2 6.1 %reduce_sum.42 = f32[320,512]{1,0:T(8,128)} reduce(f32[16,320,512]{2,1,0:T(8,128)} %bitcast.265, f32[]{:T(128)} %constant.86.clone.1), dimensions={0}, to_apply=%region_12.13 | reduce | flops 2457600 | bytes 11141124 | tf_op jit(solution)/shard_map/reduce_sum | solution.py:40
  (83 shorter events, 26.1 us)
Async XLA Ops:
  7.2 82.1 %all-gather.6.cloned.1.call-start = ((), (), s32[]{:S(2)}) async-start(), calls=%async_computation.3 | async-start | bytes 4456448 | tf_op jit(solution)/shard_map/all_gather | solution.py:19
  8.9 267.7 %reduce-scatter.2.cloned.1.call-start = ((), (), s32[]{:S(2)}) async-start(), calls=%async_computation.4 | async-start | bytes 8912896 | tf_op jit(solution)/shard_map/reduce_scatter | solution.py:242
  155.3 123.1 %copy-start.1 = (bf16[1,128,5120]{2,1,0:T(8,128)(2,1)S(1)}, bf16[1,128,5120]{2,1,0:T(8,128)(2,1)}, u32[]{:S(2)}) copy-start(bf16[1,128,5120]{2,1,0:T(8,128)(2,1)} %param.16) | copy-start | bytes 3932164
  155.3 222.8 %all-gather.8.cloned.1.call-start = ((), (), s32[]{:S(2)}) async-start(), calls=%async_computation.5 | async-start | bytes 5013504 | tf_op jit(solution)/shard_map/all_gather | solution.py:31
  278.4 8.8 %copy-start.3 = (bf16[1,16,5120]{2,1,0:T(8,128)(2,1)S(1)}, bf16[1,16,5120]{2,1,0:T(8,128)(2,1)}, u32[]{:S(2)}) copy-start(bf16[1,16,5120]{2,1,0:T(8,128)(2,1)} %param.19) | copy-start | bytes 491524
  279.9 111.8 %all-to-all-start = ((bf16[128,16,320]{0,2,1:T(8,128)(2,1)}), bf16[128,16,320]{0,2,1:T(8,128)(2,1)S(1)}, u32[]{:S(2)}, u32[]{:S(2)}) async-start(bf16[128,16,320]{0,2,1:T(8,128)(2,1)} %bitcast.50), calls=%async_computation.1 | async-start | bytes 2621440 | tf_op jit(solution)/shard_map/all_to_all | solution.py:260
  386.8 4.1 slice-start
  391.7 21.0 %all-to-all-start.1 = ((bf16[16,16,320]{2,0,1:T(8,128)(2,1)}), bf16[16,16,320]{2,0,1:T(8,128)(2,1)S(1)}, u32[]{:S(2)}, u32[]{:S(2)}) async-start(bf16[16,16,320]{2,0,1:T(8,128)(2,1)} %copy.87), calls=%async_computation.2 | async-start | bytes 393216 | tf_op jit(solution)/shard_map/all_to_all | solution.py:261
  401.7 11.0 %copy-start = (f32[256,512]{1,0:T(8,128)S(1)}, f32[256,512]{1,0:T(8,128)}, u32[]{:S(2)}) copy-start(f32[256,512]{1,0:T(8,128)} %reshape_reshape.21) | copy-start | bytes 1572868
  401.7 73.4 %all-gather.10.cloned.1.call-start = ((), (), s32[]{:S(2)}) async-start(), calls=%async_computation.6 | async-start | bytes 11141120 | tf_op jit(solution)/shard_map/all_gather | solution.py:40
  412.7 4.8 copy-start.2
Sparse Core Ops, SparseCore 0:
  11.0 78.2 all-gather.5
  155.4 121.1 reduce-scatter.1
  279.7 98.3 all-gather.7
  414.2 60.8 all-gather.9
where the time goes:
time: 489 us; the launch traced here: 488 us
  waiting for transfers between devices  349 us (71%)
  local copies, waits for them, and re-layouts  50.1 us (10%)
  matrix products  38.6 us (8%)
  starting transfers between devices  17.7 us (4%)
  other arithmetic  16.6 us (3%)
  between operations  15.3 us (3%)
    reduce_scatter x1, waiting for transfers between devices, per_device(): lax.psum_scatter(grad_terms, 'seq', scatter_dimension=0, tiled=True)  121 us
    all_gather x1, waiting for transfers between devices, gather_together(): lines, at, finished = (lax.all_gather(flat, axis), 0, [])  89.9 us
    all_gather x1, waiting for transfers between devices, sent_together(): whole = lax.all_gather(both, axis, axis=dim, tiled=True)  75.1 us
    all_gather x1, waiting for transfers between devices, over_pieces(): return lax.all_gather(array, axis).sum(0)  56.8 us
    dynamic_update_slice x8, local copies, waits for them, and re-layouts, per_device(): lax.scan(prefix_update, jnp.zeros((token_rows, KEY_VALUE_HEADS, head_repe...  13.6 us
    dot_general x8, matrix products, scores_of(): jnp.einsum('tkrd,jkd->krtj', query_rows, block, preferred_element_type=jn...  11.1 us
    all_to_all x1, starting transfers between devices, per_device(): lax.all_to_all(hidden_comp, 'seq', split_axis=1, concat_axis=0, tiled=True)  9.95 us
  transfers between devices with their start and end apart: 6, of which 5 were waited for; matrix products, arithmetic and copies ran while one was open for 6% of the time, Pallas kernels for 0%

commit v1 on v0

v1 whole, which is shorter than its diff:
```python
import functools

import jax
import jax.numpy as jnp
from jax import lax
from jax.experimental import pallas as pl
from jax.experimental.pallas import tpu as pltpu
from jax.sharding import PartitionSpec as P

HEAD = 128
KV = 4
REP = 5
SLOT = 16
PRE = 128
QR = REP * SLOT
ROWS = 4 * QR
TOK = PRE + SLOT
WIDTH = 5120
NEG_BIG = -1e30
SCALE = HEAD**-0.5
F32 = jnp.float32
BF16 = jnp.bfloat16

O_Q, O_D, O_K, O_V, O_CK, O_CV, O_END = 0, 80, 160, 288, 416, 432, 448

X_GROUPS = [[4 * x + z for x in range(4)] for z in range(4)]
Z_GROUPS = [[4 * x + z for z in range(4)] for x in range(4)]

VM = pl.BlockSpec(memory_space=pltpu.VMEM)
SM = pl.BlockSpec(memory_space=pltpu.SMEM)


def mm(a, b, ca, cb):
    return lax.dot_general(a, b, (((ca,), (cb,)), ((), ())), preferred_element_type=F32)


def kernel_call(body, outs, ins, scratch=(), name=None):
    return pl.pallas_call(
        body,
        out_shape=outs,
        in_specs=ins,
        out_specs=jax.tree.map(lambda _: VM, outs),
        scratch_shapes=list(scratch),
        name=name,
        compiler_params=pltpu.CompilerParams(vmem_limit_bytes=48 * 1024 * 1024),
    )


def live_rows(info_ref):
    t = lax.broadcasted_iota(jnp.int32, (SLOT, 1), 0)
    return (info_ref[0] < info_ref[1]) & (t < info_ref[2])


def pack_body(info_ref, q_ref, d_ref, k_ref, v_ref, ck_ref, cv_ref, out_ref):
    live = live_rows(info_ref)
    for k in range(KV):
        for r in range(REP):
            cols = pl.ds((k * REP + r) * HEAD, HEAD)
            out_ref[k, O_Q + r * SLOT : O_Q + (r + 1) * SLOT] = q_ref[:, cols]
            dout = jnp.where(live, d_ref[:, cols].astype(F32), 0.0)
            out_ref[k, O_D + r * SLOT : O_D + (r + 1) * SLOT] = dout.astype(BF16)
        cols = pl.ds(k * HEAD, HEAD)
        out_ref[k, O_K:O_V] = k_ref[:, cols]
        out_ref[k, O_V:O_CK] = v_ref[:, cols]
        out_ref[k, O_CK:O_CV] = ck_ref[:, cols]
        out_ref[k, O_CV:O_END] = cv_ref[:, cols]


def own_mask():
    key = lax.broadcasted_iota(jnp.int32, (4 * SLOT, ROWS), 0)
    row = lax.broadcasted_iota(jnp.int32, (4 * SLOT, ROWS), 1)
    same = key // SLOT == row // QR
    return same & (key % SLOT <= row % SLOT)


def rows_of(ref, lo, hi):
    return ref[:, lo:hi].reshape(-1, HEAD)


def block_q(ref):
    return rows_of(ref, O_Q, O_D)


def block_d(ref):
    return rows_of(ref, O_D, O_K)


def own_scores(a_ref, q):
    raw = mm(rows_of(a_ref, O_CK, O_CV), q, 1, 1) * SCALE
    return jnp.where(own_mask(), raw, NEG_BIG)


def stats_body(info_ref, a_ref, b1_ref, b2_ref, b3_ref, out_ref):
    z = info_ref[3]
    keys = rows_of(a_ref, O_K, O_V)
    for s, ref in enumerate((a_ref, b1_ref, b2_ref, b3_ref)):
        q = block_q(ref)
        scores = mm(keys, q, 1, 1) * SCALE
        high = jnp.max(scores, axis=0, keepdims=True)
        if s == 0:
            own = own_scores(a_ref, q)
            high = jnp.maximum(high, jnp.max(own, axis=0, keepdims=True))
        total = jnp.sum(jnp.exp(scores - high), axis=0, keepdims=True)
        if s == 0:
            total = total + jnp.sum(jnp.exp(own - high), axis=0, keepdims=True)
        zb = lax.rem(z + 4 - s, 4)
        out_ref[pl.ds(zb, 1), :] = high
        out_ref[pl.ds(zb + 4, 1), :] = total


def joined_lse(stat_refs):
    highs = [r[0:4, :] for r in stat_refs]
    totals = [r[4:8, :] for r in stat_refs]
    high = functools.reduce(jnp.maximum, highs)
    total = sum(t * jnp.exp(h - high) for h, t in zip(highs, totals))
    return high + jnp.log(total)


def value_body(info_ref, a_ref, b1_ref, b2_ref, b3_ref, s0, s1, s2, s3, vt_ref, delta_ref, lse_ref):
    z = info_ref[3]
    keys = rows_of(a_ref, O_K, O_V)
    values = rows_of(a_ref, O_V, O_CK)
    lse_ref[...] = joined_lse((s0, s1, s2, s3))
    acc = jnp.zeros((4 * PRE, HEAD), F32)
    for s, ref in enumerate((a_ref, b1_ref, b2_ref, b3_ref)):
        q = block_q(ref)
        d = block_d(ref)
        zb = lax.rem(z + 4 - s, 4)
        lse = lse_ref[pl.ds(zb, 1), :]
        probs_b = jnp.exp(mm(keys, q, 1, 1) * SCALE - lse).astype(BF16)
        acc = acc + mm(probs_b, d, 1, 0)
        dprob = mm(values, d, 1, 1)
        delta = jnp.sum(probs_b.astype(F32) * dprob, axis=0, keepdims=True)
        if s == 0:
            own_b = jnp.exp(own_scores(a_ref, q) - lse).astype(BF16)
            own_acc = mm(own_b, d, 1, 0)
            own_dprob = mm(rows_of(a_ref, O_CV, O_END), d, 1, 1)
            delta = delta + jnp.sum(own_b.astype(F32) * own_dprob, axis=0, keepdims=True)
        delta_ref[pl.ds(zb, 1), :] = delta
    for x in range(4):
        vt_ref[x, 0:PRE] = acc[x * PRE : (x + 1) * PRE].astype(BF16)
        vt_ref[x, PRE:TOK] = own_acc[x * SLOT : (x + 1) * SLOT].astype(BF16)


def grad_body(
    info_ref, a_ref, b1_ref, b2_ref, b3_ref, lse_ref, d0, d1, d2, d3, ret_ref, dk_ref, delta_ref
):
    z = info_ref[3]
    keys = rows_of(a_ref, O_K, O_V)
    values = rows_of(a_ref, O_V, O_CK)
    delta_ref[...] = (d0[...] + d1[...]) + (d2[...] + d3[...])
    acc = jnp.zeros((4 * PRE, HEAD), F32)
    for s, ref in enumerate((a_ref, b1_ref, b2_ref, b3_ref)):
        q = block_q(ref)
        d = block_d(ref)
        zb = lax.rem(z + 4 - s, 4)
        lse = lse_ref[pl.ds(zb, 1), :]
        delta = delta_ref[pl.ds(zb, 1), :]
        probs = jnp.exp(mm(keys, q, 1, 1) * SCALE - lse)
        context = mm(probs.astype(BF16), values, 0, 0)
        ds = (probs * (mm(values, d, 1, 1) - delta)).astype(BF16)
        acc = acc + mm(ds, q, 1, 0)
        dq = mm(ds, keys, 0, 0)
        if s == 0:
            own_keys = rows_of(a_ref, O_CK, O_CV)
            own_values = rows_of(a_ref, O_CV, O_END)
            own = jnp.exp(own_scores(a_ref, q) - lse)
            context = context + mm(own.astype(BF16), own_values, 0, 0)
            own_ds = (own * (mm(own_values, d, 1, 1) - delta)).astype(BF16)
            own_acc = mm(own_ds, q, 1, 0)
            dq = dq + mm(own_ds, own_keys, 0, 0)
        dq = dq * SCALE
        for x in range(4):
            ret_ref[4 * x + zb, 0:QR] = context[x * QR : (x + 1) * QR].astype(BF16)
            ret_ref[4 * x + zb, QR : 2 * QR] = dq[x * QR : (x + 1) * QR].astype(BF16)
    for x in range(4):
        dk_ref[x, 0:PRE] = (acc[x * PRE : (x + 1) * PRE] * SCALE).astype(BF16)
        dk_ref[x, PRE:TOK] = (own_acc[x * SLOT : (x + 1) * SLOT] * SCALE).astype(BF16)


def project_body(h_ref, vt_ref, out_ref):
    hidden = h_ref[...].reshape(4 * TOK, WIDTH // 4)
    for h in range(KV):
        part = mm(hidden, vt_ref[h].reshape(4 * TOK, HEAD), 0, 0)
        for z in range(4):
            for b in range(4):
                lo = z * 320 + b * 80
                out_ref[4 * h + b, z] = part[lo : lo + 80].astype(BF16)


def sum_body(in_ref, out_ref):
    total = in_ref[0].astype(F32)
    for i in range(1, in_ref.shape[0]):
        total = total + in_ref[i].astype(F32)
    out_ref[...] = total.astype(out_ref.dtype)


def unpack_body(info_ref, ret_ref, dk_ref, vt_ref, at_ref, dq_ref, ck_ref, cv_ref, pk_ref, pv_ref):
    live = live_rows(info_ref)
    x = info_ref[4]
    for k in range(KV):
        for r in range(REP):
            cols = pl.ds((k * REP + r) * HEAD, HEAD)
            lo = r * SLOT
            ctx = sum(ret_ref[4 * k + p, lo : lo + SLOT].astype(F32) for p in range(4))
            at_ref[:, cols] = jnp.where(live, ctx, 0.0).astype(BF16)
            lo = QR + r * SLOT
            dq = sum(ret_ref[4 * k + p, lo : lo + SLOT].astype(F32) for p in range(4))
            dq_ref[:, cols] = dq.astype(BF16)
        cols = pl.ds(k * HEAD, HEAD)
        pk_ref[:, cols] = dk_ref[k, 0:PRE]
        ck_ref[:, cols] = dk_ref[k, PRE:TOK]
        pv_ref[:, cols] = vt_ref[k, x, 0:PRE]
        cv_ref[:, cols] = vt_ref[k, x, PRE:TOK]


def spread_body(in_ref, out_ref):
    for h in range(KV):
        for b in range(4):
            out_ref[b * 80 : (b + 1) * 80, h * HEAD : (h + 1) * HEAD] = in_ref[4 * h + b]


def sds(shape, dtype):
    return jax.ShapeDtypeStruct(shape, dtype)


def swap(array, groups):
    return lax.all_to_all(
        array, "seq", split_axis=0, concat_axis=0, tiled=True, axis_index_groups=groups
    )


def from_others(array, groups):
    out = []
    for s in (1, 2, 3):
        pairs = [(g[i], g[(i + s) % 4]) for g in groups for i in range(4)]
        out.append(lax.ppermute(array, "seq", pairs))
    return out


def per_device(
    prefix_hidden,
    prefix_keys,
    prefix_value_rows,
    comp_hidden,
    completion_queries,
    completion_keys,
    completion_values,
    out_grad,
    counts,
    lengths,
):
    place = lax.axis_index("seq")
    info = jnp.stack([place, counts[0], lengths[0, 0], place % 4, place // 4]).astype(jnp.int32)
    packed = kernel_call(pack_body, sds((4, O_END, HEAD), BF16), [SM] + [VM] * 6, name="pack")(
        info,
        completion_queries[0],
        out_grad[0],
        prefix_keys[0],
        prefix_value_rows[0],
        completion_keys[0],
        completion_values[0],
    )
    mine = swap(packed, X_GROUPS)
    others = from_others(mine[:, O_Q:O_K], Z_GROUPS)

    hidden = jnp.concatenate([prefix_hidden[0], comp_hidden[0]], axis=0)
    hidden = jnp.transpose(hidden.reshape(TOK, 4, WIDTH // 4), (1, 0, 2))
    hidden = swap(hidden, X_GROUPS)

    stats = kernel_call(stats_body, sds((8, ROWS), F32), [SM] + [VM] * 4, name="stats")(
        info, mine, *others
    )
    stats = [stats] + from_others(stats, Z_GROUPS)
    terms, delta, lse = kernel_call(
        value_body,
        (sds((4, TOK, HEAD), BF16), sds((4, ROWS), F32), sds((4, ROWS), F32)),
        [SM] + [VM] * 8,
        name="value",
    )(info, mine, *others, *stats)

    wide = jnp.broadcast_to(terms[None], (4,) + terms.shape)
    wide = swap(wide, X_GROUPS)
    part = kernel_call(project_body, sds((16, 4, 80, HEAD), BF16), [VM] * 2, name="project")(
        hidden, wide
    )
    part = lax.all_to_all(part, "grp", split_axis=0, concat_axis=0, tiled=True)
    part = kernel_call(sum_body, sds((4, 80, HEAD), BF16), [VM], name="sum_grp")(part)
    part = swap(part, Z_GROUPS)
    part = kernel_call(sum_body, sds((80, HEAD), F32), [VM], name="sum_z")(part)
    whole = jnp.broadcast_to(part[None], (16, 80, HEAD))
    whole = lax.all_to_all(whole, "grp", split_axis=0, concat_axis=0, tiled=True)
    value_proj_grad = kernel_call(spread_body, sds((320, 512), F32), [VM], name="spread")(whole)

    deltas = [delta] + from_others(delta, Z_GROUPS)
    back, dk = kernel_call(
        grad_body,
        (sds((16, 2 * QR, HEAD), BF16), sds((4, TOK, HEAD), BF16)),
        [SM] + [VM] * 9,
        scratch=[pltpu.VMEM((4, ROWS), F32)],
        name="grad",
    )(info, mine, *others, lse, *deltas)
    back = lax.all_to_all(back, "seq", split_axis=0, concat_axis=0, tiled=True)
    dk = swap(dk, X_GROUPS)
    attn, dq, ck, cv, pk, pv = kernel_call(
        unpack_body,
        (
            sds((SLOT, 2560), BF16),
            sds((SLOT, 2560), BF16),
            sds((SLOT, 512), BF16),
            sds((SLOT, 512), BF16),
            sds((PRE, 512), BF16),
            sds((PRE, 512), BF16),
        ),
        [SM] + [VM] * 3,
        name="unpack",
    )(info, back, dk, wide)
    return attn[None], dq[None], ck[None], cv[None], pk[None], pv[None], value_proj_grad


def solution(mesh):
    rows = P("grp", "seq", None)
    return jax.shard_map(
        per_device,
        mesh=mesh,
        in_specs=(rows,) * 8 + (P("grp"), P("grp", "seq")),
        out_specs=(rows,) * 6 + (P("seq", None),),
        check_vma=False,
    )
```

time: 489 us -> 186 us (0.38)
  waiting for transfers between devices: 349 us -> 62.3 us
  local copies, waits for them, and re-layouts: 50.1 us -> 10.2 us
  blocking collectives: 0 us -> 38.9 us
  matrix products: 38.6 us -> 0 us
  starting transfers between devices: 17.7 us -> 56.1 us
  other arithmetic: 16.6 us -> 1.41 us
  Pallas kernels: 0 us -> 14.5 us
  between operations: 15.3 us -> 2.06 us
    all_gather x3 -> x0, waiting for transfers between devices: 222 us -> none  [the longest x1 89.9 us: gather_together(): lines, at, finished = (lax.all_gather(flat, axis), 0, [])]
    reduce_scatter x1 -> x0, waiting for transfers between devices: 121 us -> none  [per_device(): lax.psum_scatter(grad_terms, 'seq', scatter_dimension=0, tiled=True)]
    all_to_all x0 -> x3, blocking collectives: none -> 38.9 us  [swap(): lax.all_to_all(array, 'seq', split_axis=0, concat_axis=0, tiled=True, axi...]
    dot_general x36 -> x0, matrix products: 38.6 us -> none  [the longest x8 11.1 us: scores_of(): jnp.einsum('tkrd,jkd->krtj', query_rows, block, preferred_element_type=jn...]
    ppermute x0 -> x9, waiting for transfers between devices: none -> 28.1 us  [from_others(): out.append(lax.ppermute(array, 'seq', pairs))]
    all_to_all x2 -> x5, waiting for transfers between devices: 6.17 us -> 34.2 us  [the longest x1 17.3 us: per_device(): back = lax.all_to_all(back, 'seq', split_axis=0, concat_axis=0, tiled=True)]
    ppermute x0 -> x9, starting transfers between devices: none -> 21.4 us  [from_others(): out.append(lax.ppermute(array, 'seq', pairs))]
    all_to_all x2 -> x5, starting transfers between devices: 17.3 us -> 34.6 us  [the longest x1 14.7 us: per_device(): part = lax.all_to_all(part, 'grp', split_axis=0, concat_axis=0, tiled=True)]
  transfers between devices with their start and end apart: 6 -> 14, of which waited for: 5 -> 9; matrix products, arithmetic and copies ran while one was open for 6% -> 3% of each run, Pallas kernels for 0% -> 3%
where the time goes in v1:
time: 186 us
  waiting for transfers between devices  62.3 us (33%)
  starting transfers between devices  56.1 us (30%)
  blocking collectives  38.9 us (21%)
  Pallas kernels  14.5 us (8%)
  local copies, waits for them, and re-layouts  10.2 us (5%)
  between operations  2.06 us (1%)
    all_to_all x3, blocking collectives, swap(): lax.all_to_all(array, 'seq', split_axis=0, concat_axis=0, tiled=True, axi...  38.9 us
    ppermute x9, waiting for transfers between devices, from_others(): out.append(lax.ppermute(array, 'seq', pairs))  28.1 us
    ppermute x9, starting transfers between devices, from_others(): out.append(lax.ppermute(array, 'seq', pairs))  21.4 us
    all_to_all x1, waiting for transfers between devices, per_device(): back = lax.all_to_all(back, 'seq', split_axis=0, concat_axis=0, tiled=True)  17.3 us
    all_to_all x1, starting transfers between devices, per_device(): part = lax.all_to_all(part, 'grp', split_axis=0, concat_axis=0, tiled=True)  14.7 us
    all_to_all x1, waiting for transfers between devices, per_device(): lax.all_to_all(whole, 'grp', split_axis=0, concat_axis=0, tiled=True)  9.73 us
    all_to_all x1, starting transfers between devices, per_device(): lax.all_to_all(whole, 'grp', split_axis=0, concat_axis=0, tiled=True)  9.55 us
    all_to_all x2, waiting for transfers between devices, swap(): lax.all_to_all(array, 'seq', split_axis=0, concat_axis=0, tiled=True, axi...  7.14 us
  transfers between devices with their start and end apart: 14, of which 9 were waited for; matrix products, arithmetic and copies ran while one was open for 3% of the time, Pallas kernels for 3%

profile of v1, /device:TPU:1, one launch (start us, length us, event | category | flops | bytes accessed | tf_op | source)
XLA Modules:
  0.0 185.5 jit_solution(7232852274002309183)
XLA Ops:
  1.9 0.1 stack.15.info_ref
  2.0 0.9 copy-done
  2.9 0.9 copy-done.1
  3.8 0.9 copy-done.2
  4.7 0.9 copy-done.3
  5.6 0.7 copy-done.4
  6.3 0.7 copy-done.5
  7.0 0.6 pack.1
  7.7 12.3 %all_to_all.40.a_ref = bf16[4,448,128]{2,1,0:T(8,128)(2,1)S(1)} all-to-all(bf16[4,448,128]{2,1,0:T(8,128)(2,1)S(1)} %pack.1), channel_id=1, replica_groups={{0,4,8,12},{1,5,9,13},{2,6,10,14},{3,7,11,15},{16,20,24,28},{17,21,25,2..., dimensions={0} | all-to-all | bytes 917504 | tf_op jit(solution)/shard_map/all_to_all | solution.py:228
  19.9 6.1 %collective-permute-start.2 = (bf16[4,160,128]{2,1,0:T(8,128)(2,1)S(1)}, bf16[4,160,128]{2,1,0:T(8,128)(2,1)S(1)}, u32[]{:S(2)}, u32[]{:S(2)}) collective-permute-start(bf16[4,160,128]{2,1,0:T(8,128)(2,1)S(1)} %slice.4), channel_id=1, source_target_pairs={{0,3},{1,0},{2,1},{3,2},{4,7},{5,4},{6,5},{7,6},{8,11},{9,8},{10,9... | collective-permute-start | bytes 491528 | tf_op jit(solution)/shard_map/ppermute | solution.py:237
  26.0 1.0 collective-permute-start.1
  27.0 2.3 %collective-permute-start = (bf16[4,160,128]{2,1,0:T(8,128)(2,1)S(1)}, bf16[4,160,128]{2,1,0:T(8,128)(2,1)S(1)}, u32[]{:S(2)}, u32[]{:S(2)}) collective-permute-start(bf16[4,160,128]{2,1,0:T(8,128)(2,1)S(1)} %slice.4), channel_id=1, source_target_pairs={{0,1},{1,2},{2,3},{3,0},{4,5},{5,6},{6,7},{7,4},{8,9},{9,10},{10,1... | collective-permute-start | bytes 491528 | tf_op jit(solution)/shard_map/ppermute | solution.py:237
  29.3 1.0 collective-permute-done.2.b3_ref
  30.3 6.8 %collective-permute-done.1.b2_ref = bf16[4,160,128]{2,1,0:T(8,128)(2,1)S(1)} collective-permute-done((bf16[4,160,128]{2,1,0:T(8,128)(2,1)S(1)}, bf16[4,160,128]{2,1,0:T(8,128)(2,1)S(1)}, u32[]{:S(2)}, u32[]{:S(2)}) %collective-permute-start.1) | collective-permute-done | bytes 163872 | tf_op jit(solution)/shard_map/ppermute | solution.py:237
  37.1 2.3 %collective-permute-done.b1_ref = bf16[4,160,128]{2,1,0:T(8,128)(2,1)S(1)} collective-permute-done((bf16[4,160,128]{2,1,0:T(8,128)(2,1)S(1)}, bf16[4,160,128]{2,1,0:T(8,128)(2,1)S(1)}, u32[]{:S(2)}, u32[]{:S(2)}) %collective-permute-start) | collective-permute-done | bytes 163872 | tf_op jit(solution)/shard_map/ppermute | solution.py:237
  39.4 1.7 stats.1.s0
  41.1 0.0 copy-start.6
  41.1 4.3 %collective-permute-start.5 = (f32[8,320]{1,0:T(8,128)S(1)}, f32[8,320]{1,0:T(8,128)S(1)}, u32[]{:S(2)}, u32[]{:S(2)}) collective-permute-start(f32[8,320]{1,0:T(8,128)S(1)} %stats.1.s0), channel_id=1, source_target_pairs={{0,3},{1,0},{2,1},{3,2},{4,7},{5,4},{6,5},{7,6},{8,11},{9,8},{10,9... | collective-permute-start | bytes 30728 | tf_op jit(solution)/shard_map/ppermute | solution.py:237
  45.3 0.9 collective-permute-start.4
  46.2 1.3 collective-permute-start.3
  47.5 4.3 %collective-permute-done.4.s2 = f32[8,320]{1,0:T(8,128)S(1)} collective-permute-done((f32[8,320]{1,0:T(8,128)S(1)}, f32[8,320]{1,0:T(8,128)S(1)}, u32[]{:S(2)}, u32[]{:S(2)}) %collective-permute-start.4) | collective-permute-done | bytes 10272 | tf_op jit(solution)/shard_map/ppermute | solution.py:237
  51.8 2.3 %value.1 = (bf16[4,144,128]{2,1,0:T(8,128)(2,1)S(1)}, f32[4,320]{1,0:T(4,128)S(1)}, f32[4,320]{1,0:T(4,128)S(1)}) custom-call(s32[5]{0:T(128)S(1)} %stack.15.info_ref, bf16[4,448,128]{2,1,0:T(8,128)(2,1)S(1)} %all_to_all.40.a_ref, bf16[4,160,128]{2,1,0:T(8,128)(2,1)S(1)} %collective-permute-done.b1_ref, ...), custom_call_target="tpu_custom_call" | custom-call | tf_op jit(solution)/shard_map/value/pallas_call | solution.py:275
  54.1 0.9 broadcast_in_dim.30
  55.0 3.5 %all-to-all-start.3 = ((bf16[4,4,144,128]{3,2,1,0:T(8,128)(2,1)}), bf16[4,4,144,128]{3,2,1,0:T(8,128)(2,1)S(1)}, u32[]{:S(2)}, u32[]{:S(2)}) async-start(bf16[4,4,144,128]{3,2,1,0:T(8,128)(2,1)} %broadcast_in_dim.30), calls=%async_computation.3 | async-start | bytes 1179648 | tf_op jit(solution)/shard_map/all_to_all | solution.py:228
  58.5 0.1 concatenate.9
  58.6 1.8 copy.17
  60.4 1.5 copy.18
  61.9 1.4 maximum_bitcast_fusion
  63.3 2.4 %all-to-all-done.3.vt_ref = bf16[4,4,144,128]{3,2,1,0:T(8,128)(2,1)S(1)} async-done(((bf16[4,4,144,128]{3,2,1,0:T(8,128)(2,1)}), bf16[4,4,144,128]{3,2,1,0:T(8,128)(2,1)S(1)}, u32[]{:S(2)}, u32[]{:S(2)}) %all-to-all-start.3) | async-done | bytes 589856 | tf_op jit(solution)/shard_map/all_to_all | solution.py:228
  65.7 16.5 %all_to_all.41.h_ref = bf16[4,144,1280]{2,1,0:T(8,128)(2,1)S(1)} all-to-all(bf16[4,144,1280]{2,1,0:T(8,128)(2,1)S(1)} %maximum_bitcast_fusion), channel_id=1, replica_groups={{0,4,8,12},{1,5,9,13},{2,6,10,14},{3,7,11,15},{16,20,24,28},{17,21,25,2..., dimensions={0} | all-to-all | bytes 2949120 | tf_op jit(solution)/shard_map/all_to_all | solution.py:228
  82.3 3.0 %project.1 = bf16[16,4,80,128]{3,2,1,0:T(8,128)(2,1)} custom-call(bf16[4,144,1280]{2,1,0:T(8,128)(2,1)S(1)} %all_to_all.41.h_ref, bf16[4,4,144,128]{3,2,1,0:T(8,128)(2,1)S(1)} %all-to-all-done.3.vt_ref), custom_call_target="tpu_custom_call" | custom-call | tf_op jit(solution)/shard_map/project/pallas_call | solution.py:284
  85.2 14.7 %all-to-all-start.5 = ((bf16[16,4,80,128]{3,2,1,0:T(8,128)(2,1)}), bf16[16,4,80,128]{3,2,1,0:T(8,128)(2,1)S(1)}, u32[]{:S(2)}, u32[]{:S(2)}) async-start(bf16[16,4,80,128]{3,2,1,0:T(8,128)(2,1)} %project.1), calls=%async_computation.5 | async-start | bytes 2621440 | tf_op jit(solution)/shard_map/all_to_all | solution.py:287
  99.9 1.5 collective-permute-start.8
  101.4 2.7 %collective-permute-start.7 = (f32[4,320]{1,0:T(4,128)S(1)}, f32[4,320]{1,0:T(4,128)S(1)}, u32[]{:S(2)}, u32[]{:S(2)}) collective-permute-start(f32[4,320]{1,0:T(4,128)S(1)} %get-tuple-element.19.d0), channel_id=1, source_target_pairs={{0,2},{1,3},{2,0},{3,1},{4,6},{5,7},{6,4},{7,5},{8,10},{9,11},{10,... | collective-permute-start | bytes 15368 | tf_op jit(solution)/shard_map/ppermute | solution.py:237
  104.1 1.5 collective-permute-start.6
  105.6 13.7 %collective-permute-done.7.d2 = f32[4,320]{1,0:T(4,128)S(1)} collective-permute-done((f32[4,320]{1,0:T(4,128)S(1)}, f32[4,320]{1,0:T(4,128)S(1)}, u32[]{:S(2)}, u32[]{:S(2)}) %collective-permute-start.7) | collective-permute-done | bytes 5152 | tf_op jit(solution)/shard_map/ppermute | solution.py:237
  119.3 4.4 %grad.1 = (bf16[16,160,128]{2,1,0:T(8,128)(2,1)}, bf16[4,144,128]{2,1,0:T(8,128)(2,1)}) custom-call(s32[5]{0:T(128)S(1)} %stack.15.info_ref, bf16[4,448,128]{2,1,0:T(8,128)(2,1)S(1)} %all_to_all.40.a_ref, bf16[4,160,128]{2,1,0:T(8,128)(2,1)S(1)} %collective-permute-done.b1_ref, bf16[4,160,128]{2,1,0:T(8,128)(2,1)S(1)} %collective-permute-done.1.b2_ref, ...), custom_call_target="tpu_custom_call" | custom-call | tf_op jit(solution)/shard_map/grad/pallas_call | solution.py:296
  123.7 3.3 %all-to-all-start.2 = ((bf16[4,144,128]{2,1,0:T(8,128)(2,1)}), bf16[4,144,128]{2,1,0:T(8,128)(2,1)S(1)}, u32[]{:S(2)}, u32[]{:S(2)}) async-start(bf16[4,144,128]{2,1,0:T(8,128)(2,1)} %get-tuple-element.21), calls=%async_computation.2 | async-start | bytes 294912 | tf_op jit(solution)/shard_map/all_to_all | solution.py:228
  127.1 0.2 sum_grp.1
  127.3 4.7 %all-to-all-done.2.dk_ref = bf16[4,144,128]{2,1,0:T(8,128)(2,1)S(1)} async-done(((bf16[4,144,128]{2,1,0:T(8,128)(2,1)}), bf16[4,144,128]{2,1,0:T(8,128)(2,1)S(1)}, u32[]{:S(2)}, u32[]{:S(2)}) %all-to-all-start.2) | async-done | bytes 147488 | tf_op jit(solution)/shard_map/all_to_all | solution.py:228
  132.0 10.1 %all_to_all.42.in_ref = bf16[4,80,128]{2,1,0:T(8,128)(2,1)S(1)} all-to-all(bf16[4,80,128]{2,1,0:T(8,128)(2,1)S(1)} %sum_grp.1), channel_id=1, replica_groups={{0,1,2,3},{4,5,6,7},{8,9,10,11},{12,13,14,15},{16,17,18,19},{20,21,22,2..., dimensions={0} | all-to-all | bytes 163840 | tf_op jit(solution)/shard_map/all_to_all | solution.py:228
  142.1 3.6 %all-to-all-start.1 = ((bf16[16,160,128]{2,1,0:T(8,128)(2,1)}), bf16[16,160,128]{2,1,0:T(8,128)(2,1)S(1)}, u32[]{:S(2)}, u32[]{:S(2)}) async-start(bf16[16,160,128]{2,1,0:T(8,128)(2,1)} %get-tuple-element.20), calls=%async_computation.1 | async-start | bytes 1310720 | tf_op jit(solution)/shard_map/all_to_all | solution.py:303
  145.7 17.3 %all-to-all-done.1.ret_ref = bf16[16,160,128]{2,1,0:T(8,128)(2,1)S(1)} async-done(((bf16[16,160,128]{2,1,0:T(8,128)(2,1)}), bf16[16,160,128]{2,1,0:T(8,128)(2,1)S(1)}, u32[]{:S(2)}, u32[]{:S(2)}) %all-to-all-start.1) | async-done | bytes 655392 | tf_op jit(solution)/shard_map/all_to_all | solution.py:303
  163.1 0.9 broadcast_in_dim.37
  163.9 9.5 %all-to-all-start.7 = ((f32[16,80,128]{2,1,0:T(8,128)}), f32[16,80,128]{2,1,0:T(8,128)S(1)}, u32[]{:S(2)}, u32[]{:S(2)}) async-start(f32[16,80,128]{2,1,0:T(8,128)} %broadcast_in_dim.37), calls=%async_computation.7 | async-start | bytes 1310720 | tf_op jit(solution)/shard_map/all_to_all | solution.py:292
  173.5 1.4 unpack.1
  174.9 9.7 %all-to-all-done.7.in_ref = f32[16,80,128]{2,1,0:T(8,128)S(1)} async-done(((f32[16,80,128]{2,1,0:T(8,128)}), f32[16,80,128]{2,1,0:T(8,128)S(1)}, u32[]{:S(2)}, u32[]{:S(2)}) %all-to-all-start.7) | async-done | bytes 655392 | tf_op jit(solution)/shard_map/all_to_all | solution.py:292
  184.6 0.9 spread.1
  (15 shorter events, 0.1 us)
Async XLA Ops:
  2.0 0.9 copy-start
  2.9 0.9 copy-start.1
  3.8 0.9 copy-start.2
  4.7 0.9 copy-start.3
  5.6 0.7 copy-start.4
  6.3 0.7 copy-start.5
  19.9 10.3 %collective-permute-start.2 = (bf16[4,160,128]{2,1,0:T(8,128)(2,1)S(1)}, bf16[4,160,128]{2,1,0:T(8,128)(2,1)S(1)}, u32[]{:S(2)}, u32[]{:S(2)}) collective-permute-start(bf16[4,160,128]{2,1,0:T(8,128)(2,1)S(1)} %slice.4), channel_id=1, source_target_pairs={{0,3},{1,0},{2,1},{3,2},{4,7},{5,4},{6,5},{7,6},{8,11},{9,8},{10,9... | collective-permute-start | bytes 491528 | tf_op jit(solution)/shard_map/ppermute | solution.py:237
  26.0 11.0 %collective-permute-start.1 = (bf16[4,160,128]{2,1,0:T(8,128)(2,1)S(1)}, bf16[4,160,128]{2,1,0:T(8,128)(2,1)S(1)}, u32[]{:S(2)}, u32[]{:S(2)}) collective-permute-start(bf16[4,160,128]{2,1,0:T(8,128)(2,1)S(1)} %slice.4), channel_id=1, source_target_pairs={{0,2},{1,3},{2,0},{3,1},{4,6},{5,7},{6,4},{7,5},{8,10},{9,11},{10,... | collective-permute-start | bytes 491528 | tf_op jit(solution)/shard_map/ppermute | solution.py:237
  27.0 12.3 %collective-permute-start = (bf16[4,160,128]{2,1,0:T(8,128)(2,1)S(1)}, bf16[4,160,128]{2,1,0:T(8,128)(2,1)S(1)}, u32[]{:S(2)}, u32[]{:S(2)}) collective-permute-start(bf16[4,160,128]{2,1,0:T(8,128)(2,1)S(1)} %slice.4), channel_id=1, source_target_pairs={{0,1},{1,2},{2,3},{3,0},{4,5},{5,6},{6,7},{7,4},{8,9},{9,10},{10,1... | collective-permute-start | bytes 491528 | tf_op jit(solution)/shard_map/ppermute | solution.py:237
  41.1 17.4 %copy-start.6 = (bf16[1,16,5120]{2,1,0:T(8,128)(2,1)S(1)}, bf16[1,16,5120]{2,1,0:T(8,128)(2,1)}, u32[]{:S(2)}) copy-start(bf16[1,16,5120]{2,1,0:T(8,128)(2,1)} %param.13) | copy-start | bytes 491524
  41.1 6.4 %collective-permute-start.5 = (f32[8,320]{1,0:T(8,128)S(1)}, f32[8,320]{1,0:T(8,128)S(1)}, u32[]{:S(2)}, u32[]{:S(2)}) collective-permute-start(f32[8,320]{1,0:T(8,128)S(1)} %stats.1.s0), channel_id=1, source_target_pairs={{0,3},{1,0},{2,1},{3,2},{4,7},{5,4},{6,5},{7,6},{8,11},{9,8},{10,9... | collective-permute-start | bytes 30728 | tf_op jit(solution)/shard_map/ppermute | solution.py:237
  45.3 6.5 %collective-permute-start.4 = (f32[8,320]{1,0:T(8,128)S(1)}, f32[8,320]{1,0:T(8,128)S(1)}, u32[]{:S(2)}, u32[]{:S(2)}) collective-permute-start(f32[8,320]{1,0:T(8,128)S(1)} %stats.1.s0), channel_id=1, source_target_pairs={{0,2},{1,3},{2,0},{3,1},{4,6},{5,7},{6,4},{7,5},{8,10},{9,11},{10,... | collective-permute-start | bytes 30728 | tf_op jit(solution)/shard_map/ppermute | solution.py:237
  46.2 5.6 %collective-permute-start.3 = (f32[8,320]{1,0:T(8,128)S(1)}, f32[8,320]{1,0:T(8,128)S(1)}, u32[]{:S(2)}, u32[]{:S(2)}) collective-permute-start(f32[8,320]{1,0:T(8,128)S(1)} %stats.1.s0), channel_id=1, source_target_pairs={{0,1},{1,2},{2,3},{3,0},{4,5},{5,6},{6,7},{7,4},{8,9},{9,10},{10,1... | collective-permute-start | bytes 30728 | tf_op jit(solution)/shard_map/ppermute | solution.py:237
  55.0 10.7 %all-to-all-start.3 = ((bf16[4,4,144,128]{3,2,1,0:T(8,128)(2,1)}), bf16[4,4,144,128]{3,2,1,0:T(8,128)(2,1)S(1)}, u32[]{:S(2)}, u32[]{:S(2)}) async-start(bf16[4,4,144,128]{3,2,1,0:T(8,128)(2,1)} %broadcast_in_dim.30), calls=%async_computation.3 | async-start | bytes 1179648 | tf_op jit(solution)/shard_map/all_to_all | solution.py:228
  85.2 38.5 %all-to-all-start.5 = ((bf16[16,4,80,128]{3,2,1,0:T(8,128)(2,1)}), bf16[16,4,80,128]{3,2,1,0:T(8,128)(2,1)S(1)}, u32[]{:S(2)}, u32[]{:S(2)}) async-start(bf16[16,4,80,128]{3,2,1,0:T(8,128)(2,1)} %project.1), calls=%async_computation.5 | async-start | bytes 2621440 | tf_op jit(solution)/shard_map/all_to_all | solution.py:287
  99.9 5.7 %collective-permute-start.8 = (f32[4,320]{1,0:T(4,128)S(1)}, f32[4,320]{1,0:T(4,128)S(1)}, u32[]{:S(2)}, u32[]{:S(2)}) collective-permute-start(f32[4,320]{1,0:T(4,128)S(1)} %get-tuple-element.19.d0), channel_id=1, source_target_pairs={{0,3},{1,0},{2,1},{3,2},{4,7},{5,4},{6,5},{7,6},{8,11},{9,8},{10,9... | collective-permute-start | bytes 15368 | tf_op jit(solution)/shard_map/ppermute | solution.py:237
  101.4 17.9 %collective-permute-start.7 = (f32[4,320]{1,0:T(4,128)S(1)}, f32[4,320]{1,0:T(4,128)S(1)}, u32[]{:S(2)}, u32[]{:S(2)}) collective-permute-start(f32[4,320]{1,0:T(4,128)S(1)} %get-tuple-element.19.d0), channel_id=1, source_target_pairs={{0,2},{1,3},{2,0},{3,1},{4,6},{5,7},{6,4},{7,5},{8,10},{9,11},{10,... | collective-permute-start | bytes 15368 | tf_op jit(solution)/shard_map/ppermute | solution.py:237
  104.1 15.3 %collective-permute-start.6 = (f32[4,320]{1,0:T(4,128)S(1)}, f32[4,320]{1,0:T(4,128)S(1)}, u32[]{:S(2)}, u32[]{:S(2)}) collective-permute-start(f32[4,320]{1,0:T(4,128)S(1)} %get-tuple-element.19.d0), channel_id=1, source_target_pairs={{0,1},{1,2},{2,3},{3,0},{4,5},{5,6},{6,7},{7,4},{8,9},{9,10},{10,1... | collective-permute-start | bytes 15368 | tf_op jit(solution)/shard_map/ppermute | solution.py:237
  123.7 8.2 %all-to-all-start.2 = ((bf16[4,144,128]{2,1,0:T(8,128)(2,1)}), bf16[4,144,128]{2,1,0:T(8,128)(2,1)S(1)}, u32[]{:S(2)}, u32[]{:S(2)}) async-start(bf16[4,144,128]{2,1,0:T(8,128)(2,1)} %get-tuple-element.21), calls=%async_computation.2 | async-start | bytes 294912 | tf_op jit(solution)/shard_map/all_to_all | solution.py:228
  142.1 20.9 %all-to-all-start.1 = ((bf16[16,160,128]{2,1,0:T(8,128)(2,1)}), bf16[16,160,128]{2,1,0:T(8,128)(2,1)S(1)}, u32[]{:S(2)}, u32[]{:S(2)}) async-start(bf16[16,160,128]{2,1,0:T(8,128)(2,1)} %get-tuple-element.20), calls=%async_computation.1 | async-start | bytes 1310720 | tf_op jit(solution)/shard_map/all_to_all | solution.py:303
  163.9 20.7 %all-to-all-start.7 = ((f32[16,80,128]{2,1,0:T(8,128)}), f32[16,80,128]{2,1,0:T(8,128)S(1)}, u32[]{:S(2)}, u32[]{:S(2)}) async-start(f32[16,80,128]{2,1,0:T(8,128)} %broadcast_in_dim.37), calls=%async_computation.7 | async-start | bytes 1310720 | tf_op jit(solution)/shard_map/all_to_all | solution.py:292
